TPU v7x, 32 devices: a whole 2x2x4 slice. The times are simulated.
32 devices in a mesh: dp: 8 (over z, core), tensor: 4 (over y, x).
Axes of the slice: x: 2, y: 2, z: 4, core: 2. Of those that a mesh axis runs over, the one named last changes fastest.
Arguments:
- block_input: bfloat16 [8192, 2048], P(('dp', 'tensor')), may hold values from -6 to 6
- attention_gain: float32 [2048], replicated, may hold values from 0.1 to 1.9
- query_weight: bfloat16 [2048, 2048], P('dp', 'tensor'), may hold values from -0.125 to 0.125
- key_matrix: bfloat16 [2048, 1024], P('dp', 'tensor'), may hold values from -0.125 to 0.125
- value_matrix: bfloat16 [2048, 1024], P('dp', 'tensor'), may hold values from -0.125 to 0.125
- query_gain: float32 [128], replicated, may hold values from 0.4 to 2
- key_gain: float32 [128], replicated, may hold values from 0.4 to 2
- output_weight: bfloat16 [2048, 2048], P('tensor', 'dp'), may hold values from -1 to 1
- feed_gain: float32 [2048], replicated, may hold values from 0.1 to 1.9
- gate_weight: bfloat16 [2048, 6144], P('dp', 'tensor'), may hold values from -0.125 to 0.125
- up_weight: bfloat16 [2048, 6144], P('dp', 'tensor'), may hold values from -0.125 to 0.125
- down_weight: bfloat16 [6144, 2048], P('tensor', 'dp'), may hold values from -0.078125 to 0.078125
- out_cotangent: bfloat16 [8192, 2048], P(('dp', 'tensor')), may hold values from -6 to 6
Outputs:
- block_output: bfloat16 [8192, 2048], P(('dp', 'tensor'))
- input_gradient: bfloat16 [8192, 2048], P(('dp', 'tensor'))
- attention_gain_gradient: float32 [2048], replicated
- query_gradient: float32 [2048, 2048], P('dp', 'tensor')
- key_gradient: float32 [2048, 1024], P('dp', 'tensor')
- value_gradient: float32 [2048, 1024], P('dp', 'tensor')
- query_gain_gradient: float32 [128], replicated
- key_gain_gradient: float32 [128], replicated
- output_gradient: float32 [2048, 2048], P('tensor', 'dp')
- feed_gain_gradient: float32 [2048], replicated
- gate_gradient: float32 [2048, 6144], P('dp', 'tensor')
- up_gradient: float32 [2048, 6144], P('dp', 'tensor')
- down_gradient: float32 [6144, 2048], P('tensor', 'dp')
All inputs are finite; a program needn't handle non-finite values.
Results may differ from a plain program's by a relative error of at most 0.019.
Values may be sent and summed in bfloat16 or wider, within the bound.
A program may use at most 256 MiB of HBM per device.

v0:
```python
import jax
import jax.numpy as jnp
from jax import lax
from jax.sharding import PartitionSpec as P

SEQUENCE_LENGTH = 1024
epsilon = 1e-06
rope_base = 1000000.0


def row_scale(values):
    return lax.rsqrt(jnp.mean(values * values, axis=-1, keepdims=True) + epsilon)


def rotate_half(values):
    half_size = values.shape[-1] // 2
    return jnp.concatenate([-values[..., half_size:], values[..., :half_size]], axis=-1)


def rope_tables(positions, head_size):
    half_size = head_size // 2
    frequency = rope_base ** (-(jnp.arange(half_size).astype(jnp.float32) * 2.0 / head_size))
    angles = positions[:, None] * frequency[None, :]
    angles = jnp.concatenate([angles, angles], axis=1)
    return (jnp.cos(angles)[:, None, :], jnp.sin(angles)[:, None, :])


def contract_rows(first_operand, second_operand):
    return lax.dot_general(
        first_operand, second_operand, (((0,), (0,)), ((), ())), preferred_element_type=jnp.float32
    )


def times_transposed(first_operand, second_operand):
    return lax.dot_general(
        first_operand, second_operand, (((1,), (1,)), ((), ())), preferred_element_type=jnp.float32
    )


def simple_product(first_operand, second_operand):
    return jnp.dot(first_operand, second_operand, preferred_element_type=jnp.float32)


def masked_scores(query_block, key_seq, first_row):
    scale_factor = query_block.shape[-1] ** (-0.5)
    scores = (
        jnp.einsum("qhgd,khd->hgqk", query_block, key_seq, preferred_element_type=jnp.float32)
        * scale_factor
    )
    visible = (first_row + jnp.arange(query_block.shape[0]))[:, None] >= jnp.arange(
        key_seq.shape[0]
    )[None, :]
    return jnp.where(visible, scores, -1e30)


def attend_forward(query_block, key_seq, value_seq, first_row):
    scores = masked_scores(query_block, key_seq, first_row)
    highest = jnp.max(scores, axis=-1, keepdims=True)
    log_total = highest[..., 0] + jnp.log(jnp.sum(jnp.exp(scores - highest), axis=-1))
    weights = jnp.exp(scores - log_total[..., None]).astype(jnp.bfloat16)
    mixed_block = jnp.einsum(
        "hgqk,khd->qhgd", weights, value_seq, preferred_element_type=jnp.float32
    ).astype(jnp.bfloat16)
    return (mixed_block, log_total)


def attend_backward(
    query_block, key_seq, value_seq, mixed_block, slope_block, total_block, first_row
):
    scale_factor = query_block.shape[-1] ** (-0.5)
    scores = masked_scores(query_block, key_seq, first_row)
    weights = jnp.exp(scores - total_block[..., None])
    value_part = jnp.einsum(
        "hgqk,qhgd->khd",
        weights.astype(jnp.bfloat16),
        slope_block,
        preferred_element_type=jnp.float32,
    )
    weight_slope = jnp.einsum(
        "qhgd,khd->hgqk", slope_block, value_seq, preferred_element_type=jnp.float32
    )
    centre = jnp.transpose(
        jnp.sum(slope_block.astype(jnp.float32) * mixed_block.astype(jnp.float32), axis=-1),
        (1, 2, 0),
    )
    score_slope = (weights * (weight_slope - centre[..., None])).astype(jnp.bfloat16)
    query_part = (
        jnp.einsum("hgqk,khd->qhgd", score_slope, key_seq, preferred_element_type=jnp.float32)
        * scale_factor
    )
    key_part = (
        jnp.einsum("hgqk,qhgd->khd", score_slope, query_block, preferred_element_type=jnp.float32)
        * scale_factor
    )
    return (query_part, key_part, value_part)


def head_norm_back(turn_slope, cosine, sine, unit_values, scale_values, gain_values):
    norm_slope = turn_slope * cosine - rotate_half(turn_slope) * sine
    gain_term = jnp.sum(norm_slope * unit_values, axis=(0, 1))
    unit_slope = norm_slope * gain_values
    raw_slope = (
        scale_values
        * (unit_slope - unit_values * jnp.mean(unit_slope * unit_values, axis=-1, keepdims=True))
    ).astype(jnp.bfloat16)
    return (raw_slope.reshape(raw_slope.shape[0], -1), gain_term)


def per_device(
    block_input,
    attention_gain,
    query_weight,
    key_matrix,
    value_matrix,
    query_gain,
    key_gain,
    output_weight,
    feed_gain,
    gate_weight,
    up_weight,
    down_weight,
    out_cotangent,
):
    local_rows = block_input.shape[0]
    grouped_rows = local_rows * lax.axis_size("tensor")
    head_size = query_gain.shape[0]
    query_heads = query_weight.shape[1] // head_size
    value_heads = key_matrix.shape[1] // head_size
    grouping_width = query_heads // value_heads
    sequences = grouped_rows // SEQUENCE_LENGTH
    block_rows = min(512, SEQUENCE_LENGTH)
    block_count = SEQUENCE_LENGTH // block_rows
    cosine, sine = rope_tables(
        (jnp.arange(grouped_rows) % SEQUENCE_LENGTH).astype(jnp.float32), head_size
    )
    gathered = (
        lax.all_gather(query_weight, "dp", axis=0, tiled=True),
        lax.all_gather(key_matrix, "dp", axis=0, tiled=True),
        lax.all_gather(value_matrix, "dp", axis=0, tiled=True),
        lax.all_gather(output_weight, "dp", axis=1, tiled=True),
        lax.all_gather(gate_weight, "dp", axis=0, tiled=True),
        lax.all_gather(up_weight, "dp", axis=0, tiled=True),
        lax.all_gather(down_weight, "dp", axis=1, tiled=True),
    )
    query_full, key_full, value_full, output_full, gate_full, up_full, down_full = gathered
    input_float = block_input.astype(jnp.float32)
    first_scale = row_scale(input_float)
    first_unit = input_float * first_scale
    mixer_local = (first_unit * attention_gain).astype(jnp.bfloat16)
    attention_output_rows = lax.all_gather(mixer_local, "tensor", axis=0, tiled=True)
    query_raw = simple_product(attention_output_rows, query_full).reshape(
        grouped_rows, query_heads, head_size
    )
    unnormed_key = simple_product(attention_output_rows, key_full).reshape(
        grouped_rows, value_heads, head_size
    )
    value_token_rows = simple_product(attention_output_rows, value_full).astype(jnp.bfloat16)
    query_scale = row_scale(query_raw)
    query_unit = query_raw * query_scale
    query_normed = query_unit * query_gain
    rotated_query = (query_normed * cosine + rotate_half(query_normed) * sine).astype(jnp.bfloat16)
    key_norm_scale = row_scale(unnormed_key)
    normalized_key = unnormed_key * key_norm_scale
    key_normed = normalized_key * key_gain
    rotated_key = (key_normed * cosine + rotate_half(key_normed) * sine).astype(jnp.bfloat16)
    query_sequences = rotated_query.reshape(
        sequences, SEQUENCE_LENGTH, value_heads, grouping_width, head_size
    )
    key_sequences = rotated_key.reshape(sequences, SEQUENCE_LENGTH, value_heads, head_size)
    value_sequences = value_token_rows.reshape(sequences, SEQUENCE_LENGTH, value_heads, head_size)

    def forward_sequence(operands):
        query_seq, key_seq, value_seq = operands
        mixed_parts = []
        total_parts = []
        for block_index in range(block_count):
            first_row = block_index * block_rows
            mixed_block, log_total = attend_forward(
                query_seq[first_row : first_row + block_rows], key_seq, value_seq, first_row
            )
            mixed_parts.append(mixed_block)
            total_parts.append(log_total)
        return (jnp.concatenate(mixed_parts, axis=0), jnp.concatenate(total_parts, axis=-1))

    mixed_seqs, totals = lax.map(
        forward_sequence, (query_sequences, key_sequences, value_sequences)
    )
    mixed_rows = mixed_seqs.reshape(grouped_rows, query_heads * head_size)
    attention_sum = lax.psum_scatter(
        simple_product(
            lax.slice_in_dim(mixed_rows, 0, local_rows * lax.axis_size("tensor"), axis=0),
            output_full,
        ),
        "tensor",
        scatter_dimension=0,
        tiled=True,
    )
    hidden_state = input_float + attention_sum
    second_scale = row_scale(hidden_state)
    second_unit = hidden_state * second_scale
    feed_local = (second_unit * feed_gain).astype(jnp.bfloat16)
    feed_rows = lax.all_gather(feed_local, "tensor", axis=0, tiled=True)
    gate_values = simple_product(feed_rows, gate_full)
    up_values = simple_product(feed_rows, up_full)
    gate_sigmoid = jax.nn.sigmoid(gate_values)
    hidden_rows = (gate_values * gate_sigmoid * up_values).astype(jnp.bfloat16)
    feed_sum = lax.psum_scatter(
        simple_product(
            lax.slice_in_dim(hidden_rows, 0, local_rows * lax.axis_size("tensor"), axis=0),
            down_full,
        ).astype(jnp.bfloat16),
        "tensor",
        scatter_dimension=0,
        tiled=True,
    ).astype(jnp.float32)
    block_output = (hidden_state + feed_sum).astype(jnp.bfloat16)
    regathered = (
        lax.all_gather(query_weight, "dp", axis=0, tiled=True),
        lax.all_gather(key_matrix, "dp", axis=0, tiled=True),
        lax.all_gather(value_matrix, "dp", axis=0, tiled=True),
        lax.all_gather(output_weight, "dp", axis=1, tiled=True),
        lax.all_gather(gate_weight, "dp", axis=0, tiled=True),
        lax.all_gather(up_weight, "dp", axis=0, tiled=True),
        lax.all_gather(down_weight, "dp", axis=1, tiled=True),
    )
    query_back, key_back, value_back, output_back, gate_back, up_back, down_back = regathered
    cotangent_rows = lax.all_gather(out_cotangent, "tensor", axis=0, tiled=True)
    hidden_slope = times_transposed(cotangent_rows, down_back)
    down_grad = contract_rows(hidden_rows, cotangent_rows)
    gate_slope = (
        hidden_slope * up_values * gate_sigmoid * (1.0 + gate_values * (1.0 - gate_sigmoid))
    ).astype(jnp.bfloat16)
    up_slope = (hidden_slope * gate_values * gate_sigmoid).astype(jnp.bfloat16)
    gate_grad = contract_rows(feed_rows, gate_slope)
    up_grad = contract_rows(feed_rows, up_slope)
    gate_part = lax.slice_in_dim(gate_slope, 0, local_rows * lax.axis_size("tensor"), axis=0)
    up_part = lax.slice_in_dim(up_slope, 0, local_rows * lax.axis_size("tensor"), axis=0)
    feed_back = lax.psum_scatter(
        times_transposed(gate_part, gate_back) + times_transposed(up_part, up_back),
        "tensor",
        scatter_dimension=0,
        tiled=True,
    )
    feed_gain_term = jnp.sum(feed_back * second_unit, axis=0)
    feed_unit_slope = feed_back * feed_gain
    state_slope = out_cotangent.astype(jnp.float32) + second_scale * (
        feed_unit_slope
        - second_unit * jnp.mean(feed_unit_slope * second_unit, axis=-1, keepdims=True)
    )
    state_rounded = state_slope.astype(jnp.bfloat16)
    state_rows = lax.all_gather(state_rounded, "tensor", axis=0, tiled=True)
    mixed_gradient = times_transposed(state_rows, output_back).astype(jnp.bfloat16)
    output_grad = contract_rows(mixed_rows, state_rows)
    gradient_sequences = mixed_gradient.reshape(
        sequences, SEQUENCE_LENGTH, value_heads, grouping_width, head_size
    )

    def backward_sequence(operands):
        query_seq, key_seq, value_seq, mixed_seq, slope_seq, total_seq = operands
        key_total = jnp.zeros(key_seq.shape, jnp.float32)
        value_total = jnp.zeros(value_seq.shape, jnp.float32)
        query_parts = []
        for block_index in range(block_count):
            first_row = block_index * block_rows
            last_row = first_row + block_rows
            query_part, key_part, value_part = attend_backward(
                query_seq[first_row:last_row],
                key_seq,
                value_seq,
                mixed_seq[first_row:last_row],
                slope_seq[first_row:last_row],
                total_seq[..., first_row:last_row],
                first_row,
            )
            query_parts.append(query_part)
            key_total = key_total + key_part
            value_total = value_total + value_part
        return (jnp.concatenate(query_parts, axis=0), key_total, value_total.astype(jnp.bfloat16))

    query_slope, key_rows_gradient, value_rows_gradient = lax.map(
        backward_sequence,
        (query_sequences, key_sequences, value_sequences, mixed_seqs, gradient_sequences, totals),
    )
    query_raw_slope, query_gain_term = head_norm_back(
        query_slope.reshape(grouped_rows, query_heads, head_size),
        cosine,
        sine,
        query_unit,
        query_scale,
        query_gain,
    )
    unnormed_key_gradient, key_gain_term = head_norm_back(
        key_rows_gradient.reshape(grouped_rows, value_heads, head_size),
        cosine,
        sine,
        normalized_key,
        key_norm_scale,
        key_gain,
    )
    value_gradient_rows = value_rows_gradient.reshape(grouped_rows, value_heads * head_size)
    query_grad = contract_rows(attention_output_rows, query_raw_slope)
    key_grad = contract_rows(attention_output_rows, unnormed_key_gradient)
    value_grad = contract_rows(attention_output_rows, value_gradient_rows)
    query_part = lax.slice_in_dim(query_raw_slope, 0, local_rows * lax.axis_size("tensor"), axis=0)
    key_part = lax.slice_in_dim(
        unnormed_key_gradient, 0, local_rows * lax.axis_size("tensor"), axis=0
    )
    value_part = lax.slice_in_dim(
        value_gradient_rows, 0, local_rows * lax.axis_size("tensor"), axis=0
    )
    mixer_back = lax.psum_scatter(
        (
            times_transposed(query_part, query_back)
            + times_transposed(key_part, key_back)
            + times_transposed(value_part, value_back)
        ).astype(jnp.bfloat16),
        "tensor",
        scatter_dimension=0,
        tiled=True,
    ).astype(jnp.float32)
    attention_gain_term = jnp.sum(mixer_back * first_unit, axis=0)
    mixer_unit_slope = mixer_back * attention_gain
    input_gradient = (
        state_slope
        + first_scale
        * (
            mixer_unit_slope
            - first_unit * jnp.mean(mixer_unit_slope * first_unit, axis=-1, keepdims=True)
        )
    ).astype(jnp.bfloat16)
    weight_totals = (
        lax.psum_scatter(
            query_grad.astype(jnp.bfloat16), "dp", scatter_dimension=0, tiled=True
        ).astype(jnp.float32),
        lax.psum_scatter(
            key_grad.astype(jnp.bfloat16), "dp", scatter_dimension=0, tiled=True
        ).astype(jnp.float32),
        lax.psum_scatter(
            value_grad.astype(jnp.bfloat16), "dp", scatter_dimension=0, tiled=True
        ).astype(jnp.float32),
        lax.psum_scatter(
            output_grad.astype(jnp.bfloat16), "dp", scatter_dimension=1, tiled=True
        ).astype(jnp.float32),
        lax.psum_scatter(
            gate_grad.astype(jnp.bfloat16), "dp", scatter_dimension=0, tiled=True
        ).astype(jnp.float32),
        lax.psum_scatter(
            up_grad.astype(jnp.bfloat16), "dp", scatter_dimension=0, tiled=True
        ).astype(jnp.float32),
        lax.psum_scatter(
            down_grad.astype(jnp.bfloat16), "dp", scatter_dimension=1, tiled=True
        ).astype(jnp.float32),
    )
    gain_totals = lax.psum(
        (attention_gain_term, feed_gain_term, query_gain_term, key_gain_term), ("dp", "tensor")
    )
    return (
        block_output,
        input_gradient,
        gain_totals[0],
        weight_totals[0],
        weight_totals[1],
        weight_totals[2],
        gain_totals[2],
        gain_totals[3],
        weight_totals[3],
        gain_totals[1],
        weight_totals[4],
        weight_totals[5],
        weight_totals[6],
    )


def solution(mesh):
    in_specs = (
        P(("dp", "tensor"), None),
        P(),
        P("dp", "tensor"),
        P("dp", "tensor"),
        P("dp", "tensor"),
        P(),
        P(),
        P("tensor", "dp"),
        P(),
        P("dp", "tensor"),
        P("dp", "tensor"),
        P("tensor", "dp"),
        P(("dp", "tensor"), None),
    )
    out_specs = (
        P(("dp", "tensor"), None),
        P(("dp", "tensor"), None),
        P(),
        P("dp", "tensor"),
        P("dp", "tensor"),
        P("dp", "tensor"),
        P(),
        P(),
        P("tensor", "dp"),
        P(),
        P("dp", "tensor"),
        P("dp", "tensor"),
        P("tensor", "dp"),
    )
    return jax.shard_map(
        per_device, mesh=mesh, in_specs=in_specs, out_specs=out_specs, check_vma=False
    )
```

profile of v0, /device:TPU:0, one launch (start us, length us, event | category | flops | bytes accessed | tf_op | source)
XLA Modules:
  0.0 1226.1 jit_solution(7663798207786850853)
XLA Ops:
  9.5 2.5 fusion.16
  14.3 2.6 fusion.41
  17.2 17.3 %all-gather.16.cloned.1.call-done = bf16[2048,256]{1,0:T(8,128)(2,1)} async-done(((bf16[256,256]{1,0:T(8,128)(2,1)}), bf16[2048,256]{1,0:T(8,128)(2,1)}) %all-gather.16.cloned.1.call-update) | async-done | bytes 1048592 | tf_op jit(solution)/shard_map/all_gather | solution.py:138
  34.6 54.6 %all-gather.12.cloned.1.call-done = bf16[1024,2048]{1,0:T(8,128)(2,1)} async-done(((bf16[256,2048]{1,0:T(8,128)(2,1)}), bf16[1024,2048]{1,0:T(8,128)(2,1)}) %all-gather.12.cloned.1.call-update) | async-done | bytes 4194320 | tf_op jit(solution)/shard_map/all_gather | solution.py:150
  89.2 3.8 multiply_reduce_fusion.9
  94.4 25.6 %all-gather.18.cloned.1.call-done = bf16[2048,512]{1,0:T(8,128)(2,1)} async-done(((bf16[256,512]{1,0:T(8,128)(2,1)}), bf16[2048,512]{1,0:T(8,128)(2,1)}) %all-gather.18.cloned.1.call-update) | async-done | bytes 2097168 | tf_op jit(solution)/shard_map/all_gather | solution.py:137
  120.0 5.3 multiply_reduce_fusion.4
  135.2 2.0 exponential_reduce_fusion.1
  138.6 4.6 all-gather.14.cloned.1.call-done
  143.1 3.9 convolution_convert_fusion.11
  147.1 6.0 fusion.35
  153.2 2.4 fusion.34
  155.8 19.0 %all-gather.20.cloned.1.call-done = bf16[512,2048]{1,0:T(8,128)(2,1)} async-done(((bf16[512,256]{1,0:T(8,128)(2,1)}), bf16[512,2048]{1,0:T(8,128)(2,1)}) %all-gather.20.cloned.1.call-update) | async-done | bytes 2097168 | tf_op jit(solution)/shard_map/all_gather | solution.py:140
  174.8 7.3 fusion.54
  182.9 84.7 %reduce-scatter.12.cloned.1.call-done = f32[256,2048]{1,0:T(8,128)} async-done(((f32[1024,2048]{1,0:T(8,128)}), f32[256,2048]{1,0:T(8,128)}) %reduce-scatter.12.cloned.1.call-update) | async-done | bytes 2097168 | tf_op jit(solution)/shard_map/reduce_scatter | solution.py:189
  267.6 1.9 multiply_reduce_fusion.3
  272.9 61.1 %all-gather.24.cloned.1.call-done = bf16[2048,1536]{1,0:T(8,128)(2,1)} async-done(((bf16[256,1536]{1,0:T(8,128)(2,1)}), bf16[2048,1536]{1,0:T(8,128)(2,1)}) %all-gather.24.cloned.1.call-update) | async-done | bytes 6291472 | tf_op jit(solution)/shard_map/all_gather | solution.py:141
  334.0 53.7 %all-gather.22.cloned.1.call-done = bf16[1024,2048]{1,0:T(8,128)(2,1)} async-done(((bf16[256,2048]{1,0:T(8,128)(2,1)}), bf16[1024,2048]{1,0:T(8,128)(2,1)}) %all-gather.22.cloned.1.call-update) | async-done | bytes 4194320 | tf_op jit(solution)/shard_map/all_gather | solution.py:202
  387.6 11.9 fusion.55
  399.5 54.5 %all-gather.26.cloned.1.call-done = bf16[2048,1536]{1,0:T(8,128)(2,1)} async-done(((bf16[256,1536]{1,0:T(8,128)(2,1)}), bf16[2048,1536]{1,0:T(8,128)(2,1)}) %all-gather.26.cloned.1.call-update) | async-done | bytes 6291472 | tf_op jit(solution)/shard_map/all_gather | solution.py:142
  454.0 11.7 fusion.56
  465.8 41.2 %all-gather.30.cloned.1.call-done = bf16[1024,2048]{1,0:T(8,128)(2,1)} async-done(((bf16[256,2048]{1,0:T(8,128)(2,1)}), bf16[1024,2048]{1,0:T(8,128)(2,1)}) %all-gather.30.cloned.1.call-update) | async-done | bytes 4194320 | tf_op jit(solution)/shard_map/all_gather | solution.py:227
  506.9 66.8 %all-gather.28.cloned.1.call-done = bf16[1536,2048]{1,0:T(8,128)(2,1)} async-done(((bf16[1536,256]{1,0:T(8,128)(2,1)}), bf16[1536,2048]{1,0:T(8,128)(2,1)}) %all-gather.28.cloned.1.call-update) | async-done | bytes 6291472 | tf_op jit(solution)/shard_map/all_gather | solution.py:143
  573.7 15.9 %multiply_convert_fusion = (bf16[1024,1536]{1,0:T(8,128)(2,1)S(1)}, bf16[1024,1536]{1,0:T(8,128)(2,1)S(1)}, bf16[1024,1536]{1,0:T(8,128)(2,1)}) fusion(f32[1024,1536]{1,0:T(8,128)} %fusion.55, f32[1024,1536]{1,0:T(8,128)} %fusion.56, bf16[1024,2048]{1,0:T(8,128)(2,1)} %all-gather.30.cloned.1.call-done, bf16[1536,2048]{1,0:T(8,128)(2,1)} %all-gather.28.cloned.1.call-done), kind=kOutput, calls=%fused_computation.18 | convolution fusion | flops 6467616768 | bytes 32505856 | tf_op jit(solution)/shard_map/dot_general | solution.py:35
  589.6 11.1 fusion.57
  600.8 9.3 convolution_add_fusion
  610.2 84.6 %reduce-scatter.16.cloned.1.call-done = f32[256,2048]{1,0:T(8,128)} async-done(((f32[1024,2048]{1,0:T(8,128)}), f32[256,2048]{1,0:T(8,128)}) %reduce-scatter.16.cloned.1.call-update) | async-done | bytes 2097168 | tf_op jit(solution)/shard_map/reduce_scatter | solution.py:238
  694.8 2.3 multiply_reduce_fusion
  698.8 11.4 convolution_convert_fusion.2
  710.3 11.5 convolution_convert_fusion.1
  721.9 11.3 convolution_convert_fusion
  733.5 18.1 %all-gather.32.cloned.1.call-done = bf16[1024,2048]{1,0:T(8,128)(2,1)} async-done(((bf16[256,2048]{1,0:T(8,128)(2,1)}), bf16[1024,2048]{1,0:T(8,128)(2,1)}) %all-gather.32.cloned.1.call-update) | async-done | bytes 4194320 | tf_op jit(solution)/shard_map/all_gather | solution.py:251
  751.5 5.4 convolution_convert_fusion.8
  758.6 6.6 convolution_bitcast_fusion
  765.2 2.6 fusion.33
  768.6 2.3 convolution_convert_fusion.6
  770.9 8.7 fusion.1
  779.6 6.8 fusion.3
  786.5 3.9 convolution_bitcast_fusion.2
  790.5 2.7 fusion.31
  795.7 2.4 convolution_convert_fusion.7
  798.3 6.3 convolution_convert_fusion.4
  804.9 3.3 convolution_multiply_fusion.1
  812.2 2.3 multiply_reduce_fusion.1
  817.5 3.6 fusion.27
  822.0 3.7 convolution_convert_fusion.5
  825.9 2.7 fusion.59
  828.6 2.4 fusion.58
  831.0 3.4 add_convert_fusion
  834.8 11.1 convolution_convert_fusion.3
  846.0 2.5 convert_element_type.223
  848.5 45.3 %reduce-scatter.30.cloned.1.call-done = bf16[256,1536]{1,0:T(8,128)(2,1)} async-done(((bf16[2048,1536]{1,0:T(8,128)(2,1)}), bf16[256,1536]{1,0:T(8,128)(2,1)}) %reduce-scatter.30.cloned.1.call-update) | async-done | bytes 786448 | tf_op jit(solution)/shard_map/reduce_scatter | solution.py:347
  893.8 2.5 convert_element_type.225
  896.3 67.9 %reduce-scatter.32.cloned.1.call-done = bf16[1536,256]{1,0:T(8,128)(2,1)} async-done(((bf16[1536,2048]{1,0:T(8,128)(2,1)}), bf16[1536,256]{1,0:T(8,128)(2,1)}) %reduce-scatter.32.cloned.1.call-update) | async-done | bytes 786448 | tf_op jit(solution)/shard_map/reduce_scatter | solution.py:350
  964.2 2.4 convert_element_type.227
  966.6 30.8 %reduce-scatter.24.cloned.1.call-done = bf16[256,256]{1,0:T(8,128)(2,1)} async-done(((bf16[2048,256]{1,0:T(8,128)(2,1)}), bf16[256,256]{1,0:T(8,128)(2,1)}) %reduce-scatter.24.cloned.1.call-update) | async-done | bytes 131088 | tf_op jit(solution)/shard_map/reduce_scatter | solution.py:338
  999.0 31.4 %reduce-scatter.22.cloned.1.call-done = bf16[256,256]{1,0:T(8,128)(2,1)} async-done(((bf16[2048,256]{1,0:T(8,128)(2,1)}), bf16[256,256]{1,0:T(8,128)(2,1)}) %reduce-scatter.22.cloned.1.call-update) | async-done | bytes 131088 | tf_op jit(solution)/shard_map/reduce_scatter | solution.py:335
  1032.1 34.9 %reduce-scatter.26.cloned.1.call-done = bf16[512,256]{1,0:T(8,128)(2,1)} async-done(((bf16[512,2048]{1,0:T(8,128)(2,1)}), bf16[512,256]{1,0:T(8,128)(2,1)}) %reduce-scatter.26.cloned.1.call-update) | async-done | bytes 262160 | tf_op jit(solution)/shard_map/reduce_scatter | solution.py:341
  1068.7 35.1 %reduce-scatter.20.cloned.1.call-done = bf16[256,512]{1,0:T(8,128)(2,1)} async-done(((bf16[2048,512]{1,0:T(8,128)(2,1)}), bf16[256,512]{1,0:T(8,128)(2,1)}) %reduce-scatter.20.cloned.1.call-update) | async-done | bytes 262160 | tf_op jit(solution)/shard_map/reduce_scatter | solution.py:332
  1105.6 52.4 %reduce-scatter.18.cloned.1.call-done = bf16[256,2048]{1,0:T(8,128)(2,1)} async-done(((bf16[1024,2048]{1,0:T(8,128)(2,1)}), bf16[256,2048]{1,0:T(8,128)(2,1)}) %reduce-scatter.18.cloned.1.call-update) | async-done | bytes 1048592 | tf_op jit(solution)/shard_map/reduce_scatter | solution.py:311
  1157.9 2.1 fusion.18
  1160.0 40.1 %all-reduce = (f32[2048]{0:T(1024)}, f32[128]{0:T(128)}, f32[128]{0:T(128)}, f32[2048]{0:T(1024)}) all-reduce(f32[2048]{0:T(1024)S(1)} %get-tuple-element.53, f32[128]{0:T(128)S(1)} %reduce_sum.170, f32[128]{0:T(128)S(1)} %get-tuple-element.65, f32[2048]{0:T(1024)S(1)} %get-tuple-element.51), channel_id=1, replica_groups=mesh['dp'=8,'tensor'=4] {'dp','tensor'}, use_global_device_ids=true, to_apply=%region_19.20 | all-reduce | flops 4352 | bytes 34816 | tf_op jit(solution)/shard_map/psum | solution.py:354
  1200.1 13.7 %reduce-scatter.14.cloned.1.call-done = bf16[256,2048]{1,0:T(8,128)(2,1)} async-done(((bf16[1024,2048]{1,0:T(8,128)(2,1)}), bf16[256,2048]{1,0:T(8,128)(2,1)}) %reduce-scatter.14.cloned.1.call-update) | async-done | bytes 1048592 | tf_op jit(solution)/shard_map/reduce_scatter | solution.py:207
  1213.8 5.0 fusion.15
  (240 shorter events, 44.2 us)
Async XLA Ops:
  7.2 27.4 %all-gather.16.cloned.1.call-start = ((), (), s32[]{:S(2)}) async-start(), calls=%async_computation.13 | async-start | bytes 1179648 | tf_op jit(solution)/shard_map/all_gather | solution.py:138
  7.9 81.3 %all-gather.12.cloned.1.call-start = ((), (), s32[]{:S(2)}) async-start(), calls=%async_computation.11 | async-start | bytes 5242880 | tf_op jit(solution)/shard_map/all_gather | solution.py:150
  9.5 4.7 copy-start.54
  12.0 108.0 %all-gather.18.cloned.1.call-start = ((), (), s32[]{:S(2)}) async-start(), calls=%async_computation.14 | async-start | bytes 2359296 | tf_op jit(solution)/shard_map/all_gather | solution.py:137
  12.8 130.4 %all-gather.14.cloned.1.call-start = ((), (), s32[]{:S(2)}) async-start(), calls=%async_computation.12 | async-start | bytes 1179648 | tf_op jit(solution)/shard_map/all_gather | solution.py:139
  13.3 161.5 %all-gather.20.cloned.1.call-start = ((), (), s32[]{:S(2)}) async-start(), calls=%async_computation.15 | async-start | bytes 2359296 | tf_op jit(solution)/shard_map/all_gather | solution.py:140
  13.9 253.7 %reduce-scatter.12.cloned.1.call-start = ((), (), s32[]{:S(2)}) async-start(), calls=%async_computation.16 | async-start | bytes 10485760 | tf_op jit(solution)/shard_map/reduce_scatter | solution.py:189
  14.2 138.9 %copy-start.25 = (pred[512,1024]{0,1:T(8,128)(4,1)}, pred[512,1024]{0,1:T(8,128)(4,1)S(1)}, u32[]{:S(2)}) copy-start(pred[512,1024]{0,1:T(8,128)(4,1)S(1)} %iota_compare_fusion.1) | copy-start | bytes 1572868
  16.8 110.8 %copy-start.14 = (f32[1024,128]{0,1:T(8,128)}, f32[1024,128]{0,1:T(8,128)S(1)}, u32[]{:S(2)}) copy-start(f32[1024,128]{0,1:T(8,128)S(1)} %get-tuple-element.98) | copy-start | bytes 1572868
  17.2 129.9 %copy-start.27 = (pred[512,1024]{0,1:T(8,128)(4,1)}, pred[512,1024]{0,1:T(8,128)(4,1)S(1)}, u32[]{:S(2)}) copy-start(pred[512,1024]{0,1:T(8,128)(4,1)S(1)} %iota_compare_fusion) | copy-start | bytes 1572868
  17.2 75.8 %copy-start.58 = (f32[128]{0:T(128)S(1)}, f32[128]{0:T(128)}, u32[]{:S(2)}) copy-start(f32[128]{0:T(128)} %param.19) | copy-start | bytes 1540
  93.0 34.6 %copy-start.7 = (f32[1024,256]{0,1:T(8,128)}, f32[1024,256]{0,1:T(8,128)S(1)}, u32[]{:S(2)}) copy-start(f32[1024,256]{0,1:T(8,128)S(1)} %get-tuple-element.100) | copy-start | bytes 3145732
  93.0 34.6 %copy-start.50 = (f32[1024,2]{0,1:T(2,128)}, f32[1024,2]{0,1:T(2,128)S(1)}, u32[]{:S(2)}) copy-start(f32[1024,2]{0,1:T(2,128)S(1)} %add_rsqrt_fusion.1) | copy-start | bytes 24580
  94.4 30.9 %copy-start.56 = (f32[128]{0:T(128)S(1)}, f32[128]{0:T(128)}, u32[]{:S(2)}) copy-start(f32[128]{0:T(128)} %param.18) | copy-start | bytes 1540
  127.6 5.9 copy-start.29
  128.4 5.1 copy-start.20
  143.1 10.0 slice-start
  147.1 6.1 copy-start.65
  147.1 6.1 slice-start.1
  155.6 26.5 %copy-start.36 = (bf16[512,2,2,128]{0,3,2,1:T(8,128)(2,1)}, bf16[512,2,2,128]{0,3,2,1:T(8,128)(2,1)S(1)}, u32[]{:S(2)}) copy-start(bf16[512,2,2,128]{0,3,2,1:T(8,128)(2,1)S(1)} %fusion.34) | copy-start | bytes 1572868
  155.8 26.3 %copy-start.42 = (bf16[1024,2,2,128]{0,3,2,1:T(8,128)(2,1)}, bf16[1024,2,2,128]{0,3,2,1:T(8,128)(2,1)S(1)}, u32[]{:S(2)}) copy-start(bf16[1024,2,2,128]{0,3,2,1:T(8,128)(2,1)S(1)} %pad_maximum_fusion.1) | copy-start | bytes 3145732
  182.1 85.5 %copy-start.5 = (bf16[256,2048]{1,0:T(8,128)(2,1)S(1)}, bf16[256,2048]{1,0:T(8,128)(2,1)}, u32[]{:S(2)}) copy-start(bf16[256,2048]{1,0:T(8,128)(2,1)} %param.13) | copy-start | bytes 3145732
  182.1 87.4 %copy-start.52 = (f32[2048]{0:T(1024)S(1)}, f32[2048]{0:T(1024)}, u32[]{:S(2)}) copy-start(f32[2048]{0:T(1024)} %param.21) | copy-start | bytes 24580
  182.1 151.8 %all-gather.24.cloned.1.call-start = ((), (), s32[]{:S(2)}) async-start(), calls=%async_computation.18 | async-start | bytes 7077888 | tf_op jit(solution)/shard_map/all_gather | solution.py:141
  182.9 204.8 %all-gather.22.cloned.1.call-start = ((), (), s32[]{:S(2)}) async-start(), calls=%async_computation.17 | async-start | bytes 5242880 | tf_op jit(solution)/shard_map/all_gather | solution.py:202
  270.8 183.2 %all-gather.26.cloned.1.call-start = ((), (), s32[]{:S(2)}) async-start(), calls=%async_computation.19 | async-start | bytes 7077888 | tf_op jit(solution)/shard_map/all_gather | solution.py:142
  271.5 235.4 %all-gather.30.cloned.1.call-start = ((), (), s32[]{:S(2)}) async-start(), calls=%async_computation.22 | async-start | bytes 5242880 | tf_op jit(solution)/shard_map/all_gather | solution.py:227
  272.1 301.6 %all-gather.28.cloned.1.call-start = ((), (), s32[]{:S(2)}) async-start(), calls=%async_computation.20 | async-start | bytes 7077888 | tf_op jit(solution)/shard_map/all_gather | solution.py:143
  272.8 422.0 %reduce-scatter.16.cloned.1.call-start = ((), (), s32[]{:S(2)}) async-start(), calls=%async_computation.23 | async-start | bytes 10485760 | tf_op jit(solution)/shard_map/reduce_scatter | solution.py:238
  589.6 11.1 copy-start.67
  589.6 11.2 copy-start.68
  589.6 11.2 copy-start.60
  610.1 87.0 %copy-start.22 = (bf16[256,2048]{1,0:T(8,128)(2,1)S(1)}, bf16[256,2048]{1,0:T(8,128)(2,1)}, u32[]{:S(2)}) copy-start(bf16[256,2048]{1,0:T(8,128)(2,1)} %param.25) | copy-start | bytes 3145732
  610.2 141.4 %all-gather.32.cloned.1.call-start = ((), (), s32[]{:S(2)}) async-start(), calls=%async_computation.24 | async-start | bytes 5242880 | tf_op jit(solution)/shard_map/all_gather | solution.py:251
  698.8 147.2 %reduce-scatter.28.cloned.1.call-start = ((), (), s32[]{:S(2)}) async-start(), calls=%async_computation.30 | async-start | bytes 7077888 | tf_op jit(solution)/shard_map/reduce_scatter | solution.py:344
  710.3 183.5 %reduce-scatter.30.cloned.1.call-start = ((), (), s32[]{:S(2)}) async-start(), calls=%async_computation.31 | async-start | bytes 7077888 | tf_op jit(solution)/shard_map/reduce_scatter | solution.py:347
  721.9 242.3 %reduce-scatter.32.cloned.1.call-start = ((), (), s32[]{:S(2)}) async-start(), calls=%async_computation.32 | async-start | bytes 7077888 | tf_op jit(solution)/shard_map/reduce_scatter | solution.py:350
  733.2 23.7 %copy-start.35 = (bf16[512,2,2,128]{0,3,2,1:T(8,128)(2,1)S(1)}, bf16[512,2,2,128]{0,3,2,1:T(8,128)(2,1)}, u32[]{:S(2)}) copy-start(bf16[512,2,2,128]{0,3,2,1:T(8,128)(2,1)} %copy-done.34) | copy-start | bytes 1572868
  733.2 264.2 %reduce-scatter.24.cloned.1.call-start = ((), (), s32[]{:S(2)}) async-start(), calls=%async_computation.28 | async-start | bytes 1179648 | tf_op jit(solution)/shard_map/reduce_scatter | solution.py:338
  751.5 7.0 copy-start.28
  751.5 13.6 %slice-start.2 = ((s8[8388608]{0:T(1024)(128)(4,1)}), s8[4194304]{0:T(1024)(128)(4,1)S(1)}, s32[]{:S(2)}) async-start(s8[8388608]{0:T(1024)(128)(4,1)} %bitcast.226), calls=%async_computation.35 | async-start | bytes 8388608
  756.9 8.2 slice-start.3
  758.5 6.6 copy-start.47
  758.5 6.6 copy-start.45
  758.5 6.6 copy-start.26
  765.2 3.4 copy-start.61
  770.9 8.7 copy-start.46
  770.9 8.7 copy-start.66
  779.6 6.9 copy-start.31
  786.4 244.0 %reduce-scatter.22.cloned.1.call-start = ((), (), s32[]{:S(2)}) async-start(), calls=%async_computation.27 | async-start | bytes 1179648 | tf_op jit(solution)/shard_map/reduce_scatter | solution.py:335
  786.5 3.9 copy-start.19
  798.2 6.7 copy-start.57
  798.2 6.7 copy-start.49
  798.2 268.7 %reduce-scatter.26.cloned.1.call-start = ((), (), s32[]{:S(2)}) async-start(), calls=%async_computation.29 | async-start | bytes 2359296 | tf_op jit(solution)/shard_map/reduce_scatter | solution.py:341
  804.6 299.2 %reduce-scatter.20.cloned.1.call-start = ((), (), s32[]{:S(2)}) async-start(), calls=%async_computation.26 | async-start | bytes 2359296 | tf_op jit(solution)/shard_map/reduce_scatter | solution.py:332
  804.9 3.7 copy-start.16
  804.9 3.8 copy-start.21
  817.5 4.5 copy-start.63
  822.0 3.8 copy-start.33
  825.8 332.1 %reduce-scatter.18.cloned.1.call-start = ((), (), s32[]{:S(2)}) async-start(), calls=%async_computation.25 | async-start | bytes 5242880 | tf_op jit(solution)/shard_map/reduce_scatter | solution.py:311
  834.4 379.4 %reduce-scatter.14.cloned.1.call-start = ((), (), s32[]{:S(2)}) async-start(), calls=%async_computation.21 | async-start | bytes 5242880 | tf_op jit(solution)/shard_map/reduce_scatter | solution.py:207
  845.9 312.0 %copy-start.6 = (bf16[256,2048]{1,0:T(8,128)(2,1)S(1)}, bf16[256,2048]{1,0:T(8,128)(2,1)}, u32[]{:S(2)}) copy-start(bf16[256,2048]{1,0:T(8,128)(2,1)} %param.13) | copy-start | bytes 3145732
  845.9 312.0 %copy-start.53 = (f32[2048]{0:T(1024)S(1)}, f32[2048]{0:T(1024)}, u32[]{:S(2)}) copy-start(f32[2048]{0:T(1024)} %param.14) | copy-start | bytes 24580
  845.9 312.0 %copy-start.55 = (f32[256]{0:T(256)S(1)}, f32[256]{0:T(256)}, u32[]{:S(2)}) copy-start(f32[256]{0:T(256)} %copy-done.54) | copy-start | bytes 3076
  (31 other events, 70.0 us)
Sparse Core Ops, SparseCore 0:
  9.6 24.9 all-gather.15
  37.0 52.1 all-gather.11
  90.8 29.1 all-gather.17
  121.5 21.6 all-gather.13
  144.6 30.1 all-gather.19
  182.2 85.2 reduce-scatter.11
  269.2 64.7 all-gather.23
  336.4 51.2 all-gather.21
  389.3 64.6 all-gather.25
  455.7 51.2 all-gather.29
  508.5 65.1 all-gather.27
  610.3 84.4 reduce-scatter.15
  698.9 52.5 all-gather.31
  753.7 69.7 reduce-scatter.27
  825.6 68.1 reduce-scatter.29
  896.0 68.1 reduce-scatter.31
  966.3 31.0 reduce-scatter.23
  999.5 30.8 reduce-scatter.21
  1032.7 34.1 reduce-scatter.25
  1069.1 34.6 reduce-scatter.19
  1106.8 51.1 reduce-scatter.17
  1160.9 52.8 reduce-scatter.13
where the time goes:
time: 1240 us; the launch traced here: 1230 us
  waiting for transfers between devices  902 us (73%)
  matrix products  201 us (16%)
  other arithmetic  53.5 us (4%)
  blocking collectives  40.1 us (3%)
  between operations  16 us (1%)
    reduce_scatter x1, waiting for transfers between devices, per_device(): lax.psum_scatter(simple_product(lax.slice_in_dim(mixed_rows, 0, local_row...  84.7 us
    reduce_scatter x1, waiting for transfers between devices, per_device(): lax.psum_scatter(times_transposed(gate_part, gate_back) + times_transpose...  84.6 us
    reduce_scatter x1, waiting for transfers between devices, per_device(): lax.psum_scatter(down_grad.astype(jnp.bfloat16), 'dp', scatter_dimension=...  67.9 us
    all_gather x1, waiting for transfers between devices, per_device(): lax.all_gather(down_weight, 'dp', axis=1, tiled=True)  66.8 us
    all_gather x1, waiting for transfers between devices, per_device(): lax.all_gather(gate_weight, 'dp', axis=0, tiled=True)  61.1 us
    dot_general x7, matrix products, simple_product(): jnp.dot(first_operand, second_operand, preferred_element_type=jnp.float32)  55 us
    all_gather x1, waiting for transfers between devices, per_device(): lax.all_gather(mixer_local, 'tensor', axis=0, tiled=True)  54.6 us
    all_gather x1, waiting for transfers between devices, per_device(): lax.all_gather(up_weight, 'dp', axis=0, tiled=True)  54.5 us
  transfers between devices with their start and end apart: 22, of which 21 were waited for; matrix products, arithmetic and copies ran while one was open for 17% of the time, Pallas kernels for 0%

commit v1 on v0

--- a/solution.py
+++ b/solution.py
@@ -147,7 +147,32 @@
     first_scale = row_scale(input_float)
     first_unit = input_float * first_scale
     mixer_local = (first_unit * attention_gain).astype(jnp.bfloat16)
-    attention_output_rows = lax.all_gather(mixer_local, "tensor", axis=0, tiled=True)
+    frame_out = jax.lax.axis_size("tensor")
+    carry, carry_out, reached = (frame_out, jax.lax.axis_index("tensor"), mixer_local.shape[0])
+    grid = []
+    for dev_i in range(carry):
+        grid.append((dev_i, (dev_i + 1) % carry))
+    inbox = []
+    for dev_i in range(carry):
+        inbox.append((dev_i, (dev_i - 1) % carry))
+    attention_output_rows = jnp.zeros(
+        (*mixer_local.shape[:0], carry * reached, *mixer_local.shape[0 + 1 :]), mixer_local.dtype
+    )
+    attention_output_rows = lax.dynamic_update_slice_in_dim(
+        attention_output_rows, mixer_local, carry_out * reached, axis=0
+    )
+    current_value = piece_out = mixer_local
+    then = carry // 2
+    for w in range(1, then + 1):
+        current_value = jax.lax.ppermute(current_value, "tensor", grid)
+        attention_output_rows = lax.dynamic_update_slice_in_dim(
+            attention_output_rows, current_value, (carry_out - w) % carry * reached, axis=0
+        )
+        if w < carry - then:
+            piece_out = jax.lax.ppermute(piece_out, "tensor", inbox)
+            attention_output_rows = lax.dynamic_update_slice_in_dim(
+                attention_output_rows, piece_out, (carry_out + w) % carry * reached, axis=0
+            )
     query_raw = simple_product(attention_output_rows, query_full).reshape(
         grouped_rows, query_heads, head_size
     )

time: 1240 us -> 1180 us (0.952)
  waiting for transfers between devices: 902 us -> 836 us
    ppermute x0 -> x3, waiting for transfers between devices: none -> 59.7 us  [the longest x2 42.8 us: per_device(): current_value = jax.lax.ppermute(current_value, 'tensor', grid)]
    all_gather x1 -> x0, waiting for transfers between devices: 54.6 us -> none  [per_device(): lax.all_gather(mixer_local, 'tensor', axis=0, tiled=True)]
    all_gather x1, waiting for transfers between devices: 25.6 us -> 0.01 us  [per_device(): lax.all_gather(query_weight, 'dp', axis=0, tiled=True)]
    all_gather x1, waiting for transfers between devices: 19 us -> 0.02 us  [per_device(): lax.all_gather(output_weight, 'dp', axis=1, tiled=True)]
    all_gather x1, waiting for transfers between devices: 17.3 us -> 0.01 us  [per_device(): lax.all_gather(key_matrix, 'dp', axis=0, tiled=True)]
  transfers between devices with their start and end apart: 22 -> 24, of which waited for: 21 -> 19; matrix products, arithmetic and copies ran while one was open for 17% -> 18% of each run, Pallas kernels for 0% -> 0%
where the time goes in v1:
time: 1180 us; the launch traced here: 1170 us
  waiting for transfers between devices  836 us (71%)
  matrix products  206 us (17%)
  other arithmetic  53.1 us (4%)
  blocking collectives  40.1 us (3%)
  local copies, waits for them, and re-layouts  17.1 us (1%)
  between operations  16 us (1%)
    reduce_scatter x1, waiting for transfers between devices, per_device(): lax.psum_scatter(simple_product(lax.slice_in_dim(mixed_rows, 0, local_row...  86.4 us
    reduce_scatter x1, waiting for transfers between devices, per_device(): lax.psum_scatter(times_transposed(gate_part, gate_back) + times_transpose...  84.6 us
    reduce_scatter x1, waiting for transfers between devices, per_device(): lax.psum_scatter(down_grad.astype(jnp.bfloat16), 'dp', scatter_dimension=...  67.9 us
    all_gather x1, waiting for transfers between devices, per_device(): lax.all_gather(down_weight, 'dp', axis=1, tiled=True)  66.6 us
    all_gather x1, waiting for transfers between devices, per_device(): lax.all_gather(gate_weight, 'dp', axis=0, tiled=True)  60.9 us
    dot_general x7, matrix products, simple_product(): jnp.dot(first_operand, second_operand, preferred_element_type=jnp.float32)  56.3 us
    dot_general x7, matrix products, contract_rows(): lax.dot_general(first_operand, second_operand, (((0,), (0,)), ((), ())),...  55.7 us
    all_gather x1, waiting for transfers between devices, per_device(): lax.all_gather(up_weight, 'dp', axis=0, tiled=True)  54.5 us
  transfers between devices with their start and end apart: 24, of which 19 were waited for; matrix products, arithmetic and copies ran while one was open for 18% of the time, Pallas kernels for 0%

profile of v1, /device:TPU:0, one launch (start us, length us, event | category | flops | bytes accessed | tf_op | source)
XLA Modules:
  0.0 1174.8 jit_solution(12900673395106049549)
XLA Ops:
  11.0 2.6 broadcast_in_dim.69
  15.2 3.0 collective-permute-start
  19.3 24.0 %collective-permute-done = bf16[256,2048]{1,0:T(8,128)(2,1)S(1)} collective-permute-done((bf16[256,2048]{1,0:T(8,128)(2,1)}, bf16[256,2048]{1,0:T(8,128)(2,1)S(1)}, u32[]{:S(2)}, u32[]{:S(2)}) %collective-permute-start) | collective-permute-done | bytes 1048608 | tf_op jit(solution)/shard_map/ppermute | solution.py:167
  49.5 16.9 %collective-permute-done.1 = bf16[256,2048]{1,0:T(8,128)(2,1)} collective-permute-done((bf16[256,2048]{1,0:T(8,128)(2,1)}, bf16[256,2048]{1,0:T(8,128)(2,1)}, u32[]{:S(2)}, u32[]{:S(2)}) %collective-permute-start.1) | collective-permute-done | bytes 1048608 | tf_op jit(solution)/shard_map/ppermute | solution.py:172
  66.4 2.4 constant_dynamic-update-slice_fusion.1
  68.8 18.7 %collective-permute-done.2 = bf16[256,2048]{1,0:T(8,128)(2,1)} collective-permute-done((bf16[256,2048]{1,0:T(8,128)(2,1)S(1)}, bf16[256,2048]{1,0:T(8,128)(2,1)}, u32[]{:S(2)}, u32[]{:S(2)}) %collective-permute-start.2) | collective-permute-done | bytes 1048608 | tf_op jit(solution)/shard_map/ppermute | solution.py:167
  87.5 2.3 constant_dynamic-update-slice_fusion
  89.8 3.8 multiply_reduce_fusion.9
  95.6 4.9 convolution_convert_fusion.11
  100.4 5.3 multiply_reduce_fusion.4
  110.7 2.0 exponential_reduce_fusion
  116.4 2.4 fusion.35
  118.8 2.4 fusion.34
  121.5 7.7 fusion.55
  129.8 86.4 %reduce-scatter.12.cloned.1.call-done = f32[256,2048]{1,0:T(8,128)} async-done(((f32[1024,2048]{1,0:T(8,128)}), f32[256,2048]{1,0:T(8,128)}) %reduce-scatter.12.cloned.1.call-update) | async-done | bytes 2097168 | tf_op jit(solution)/shard_map/reduce_scatter | solution.py:214
  221.5 60.9 %all-gather.21.cloned.1.call-done = bf16[2048,1536]{1,0:T(8,128)(2,1)} async-done(((bf16[256,1536]{1,0:T(8,128)(2,1)}), bf16[2048,1536]{1,0:T(8,128)(2,1)}) %all-gather.21.cloned.1.call-update) | async-done | bytes 6291472 | tf_op jit(solution)/shard_map/all_gather | solution.py:141
  282.4 53.7 %all-gather.19.cloned.1.call-done = bf16[1024,2048]{1,0:T(8,128)(2,1)} async-done(((bf16[256,2048]{1,0:T(8,128)(2,1)}), bf16[1024,2048]{1,0:T(8,128)(2,1)}) %all-gather.19.cloned.1.call-update) | async-done | bytes 4194320 | tf_op jit(solution)/shard_map/all_gather | solution.py:227
  336.1 11.9 %fusion.56 = f32[1024,1536]{1,0:T(8,128)} fusion(bf16[1024,2048]{1,0:T(8,128)(2,1)} %all-gather.19.cloned.1.call-done, bf16[2048,1536]{1,0:T(8,128)(2,1)} %all-gather.21.cloned.1.call-done), kind=kOutput, calls=%fused_computation.142 | convolution fusion | flops 6442450944 | bytes 16777216 | tf_op jit(solution)/shard_map/dot_general | solution.py:41
  348.0 54.5 %all-gather.23.cloned.1.call-done = bf16[2048,1536]{1,0:T(8,128)(2,1)} async-done(((bf16[256,1536]{1,0:T(8,128)(2,1)}), bf16[2048,1536]{1,0:T(8,128)(2,1)}) %all-gather.23.cloned.1.call-update) | async-done | bytes 6291472 | tf_op jit(solution)/shard_map/all_gather | solution.py:142
  402.5 11.7 fusion.57
  414.1 41.4 %all-gather.27.cloned.1.call-done = bf16[1024,2048]{1,0:T(8,128)(2,1)} async-done(((bf16[256,2048]{1,0:T(8,128)(2,1)}), bf16[1024,2048]{1,0:T(8,128)(2,1)}) %all-gather.27.cloned.1.call-update) | async-done | bytes 4194320 | tf_op jit(solution)/shard_map/all_gather | solution.py:252
  455.6 66.6 %all-gather.25.cloned.1.call-done = bf16[1536,2048]{1,0:T(8,128)(2,1)} async-done(((bf16[1536,256]{1,0:T(8,128)(2,1)}), bf16[1536,2048]{1,0:T(8,128)(2,1)}) %all-gather.25.cloned.1.call-update) | async-done | bytes 6291472 | tf_op jit(solution)/shard_map/all_gather | solution.py:143
  522.2 15.9 %multiply_convert_fusion = (bf16[1024,1536]{1,0:T(8,128)(2,1)S(1)}, bf16[1024,1536]{1,0:T(8,128)(2,1)S(1)}, bf16[1024,1536]{1,0:T(8,128)(2,1)}) fusion(f32[1024,1536]{1,0:T(8,128)} %fusion.56, f32[1024,1536]{1,0:T(8,128)} %fusion.57, bf16[1024,2048]{1,0:T(8,128)(2,1)} %all-gather.27.cloned.1.call-done, bf16[1536,2048]{1,0:T(8,128)(2,1)} %all-gather.25.cloned.1.call-done), kind=kOutput, calls=%fused_computation.18 | convolution fusion | flops 6467616768 | bytes 32505856 | tf_op jit(solution)/shard_map/dot_general | solution.py:35
  538.1 11.1 fusion.58
  549.3 9.4 convolution_add_fusion
  558.8 84.6 %reduce-scatter.16.cloned.1.call-done = f32[256,2048]{1,0:T(8,128)} async-done(((f32[1024,2048]{1,0:T(8,128)}), f32[256,2048]{1,0:T(8,128)}) %reduce-scatter.16.cloned.1.call-update) | async-done | bytes 2097168 | tf_op jit(solution)/shard_map/reduce_scatter | solution.py:263
  643.3 2.3 multiply_reduce_fusion
  647.4 11.5 convolution_convert_fusion.2
  659.0 11.5 convolution_convert_fusion.1
  670.5 11.3 convolution_convert_fusion
  682.1 18.0 %all-gather.29.cloned.1.call-done = bf16[1024,2048]{1,0:T(8,128)(2,1)} async-done(((bf16[256,2048]{1,0:T(8,128)(2,1)}), bf16[1024,2048]{1,0:T(8,128)(2,1)}) %all-gather.29.cloned.1.call-update) | async-done | bytes 4194320 | tf_op jit(solution)/shard_map/all_gather | solution.py:276
  700.1 5.4 convolution_convert_fusion.8
  707.1 6.6 convolution_bitcast_fusion
  713.8 2.6 fusion.33
  717.2 4.6 convolution_convert_fusion.6
  721.8 8.6 fusion.1
  730.4 6.8 fusion.3
  737.4 3.9 convolution_bitcast_fusion.2
  741.3 2.7 fusion.31
  745.9 4.6 convolution_convert_fusion.7
  750.6 6.3 convolution_convert_fusion.4
  757.3 3.3 convolution_multiply_fusion.1
  764.6 2.3 multiply_reduce_fusion.1
  767.0 2.0 maximum_multiply_fusion.1
  769.9 3.4 fusion.27
  774.2 6.0 convolution_convert_fusion.5
  780.3 2.7 fusion.60
  783.0 2.4 fusion.59
  785.5 3.4 add_convert_fusion
  789.2 11.2 convolution_convert_fusion.3
  800.4 2.5 convert_element_type.223
  803.0 39.6 %reduce-scatter.30.cloned.1.call-done = bf16[256,1536]{1,0:T(8,128)(2,1)} async-done(((bf16[2048,1536]{1,0:T(8,128)(2,1)}), bf16[256,1536]{1,0:T(8,128)(2,1)}) %reduce-scatter.30.cloned.1.call-update) | async-done | bytes 786448 | tf_op jit(solution)/shard_map/reduce_scatter | solution.py:372
  842.5 2.5 convert_element_type.225
  845.0 67.9 %reduce-scatter.32.cloned.1.call-done = bf16[1536,256]{1,0:T(8,128)(2,1)} async-done(((bf16[1536,2048]{1,0:T(8,128)(2,1)}), bf16[1536,256]{1,0:T(8,128)(2,1)}) %reduce-scatter.32.cloned.1.call-update) | async-done | bytes 786448 | tf_op jit(solution)/shard_map/reduce_scatter | solution.py:375
  912.9 2.4 convert_element_type.227
  915.3 30.8 %reduce-scatter.24.cloned.1.call-done = bf16[256,256]{1,0:T(8,128)(2,1)} async-done(((bf16[2048,256]{1,0:T(8,128)(2,1)}), bf16[256,256]{1,0:T(8,128)(2,1)}) %reduce-scatter.24.cloned.1.call-update) | async-done | bytes 131088 | tf_op jit(solution)/shard_map/reduce_scatter | solution.py:363
  947.7 31.3 %reduce-scatter.22.cloned.1.call-done = bf16[256,256]{1,0:T(8,128)(2,1)} async-done(((bf16[2048,256]{1,0:T(8,128)(2,1)}), bf16[256,256]{1,0:T(8,128)(2,1)}) %reduce-scatter.22.cloned.1.call-update) | async-done | bytes 131088 | tf_op jit(solution)/shard_map/reduce_scatter | solution.py:360
  980.7 34.8 %reduce-scatter.26.cloned.1.call-done = bf16[512,256]{1,0:T(8,128)(2,1)} async-done(((bf16[512,2048]{1,0:T(8,128)(2,1)}), bf16[512,256]{1,0:T(8,128)(2,1)}) %reduce-scatter.26.cloned.1.call-update) | async-done | bytes 262160 | tf_op jit(solution)/shard_map/reduce_scatter | solution.py:366
  1017.3 35.2 %reduce-scatter.20.cloned.1.call-done = bf16[256,512]{1,0:T(8,128)(2,1)} async-done(((bf16[2048,512]{1,0:T(8,128)(2,1)}), bf16[256,512]{1,0:T(8,128)(2,1)}) %reduce-scatter.20.cloned.1.call-update) | async-done | bytes 262160 | tf_op jit(solution)/shard_map/reduce_scatter | solution.py:357
  1054.3 52.3 %reduce-scatter.18.cloned.1.call-done = bf16[256,2048]{1,0:T(8,128)(2,1)} async-done(((bf16[1024,2048]{1,0:T(8,128)(2,1)}), bf16[256,2048]{1,0:T(8,128)(2,1)}) %reduce-scatter.18.cloned.1.call-update) | async-done | bytes 1048592 | tf_op jit(solution)/shard_map/reduce_scatter | solution.py:336
  1106.6 2.1 fusion.18
  1108.7 40.1 %all-reduce = (f32[2048]{0:T(1024)}, f32[128]{0:T(128)}, f32[128]{0:T(128)}, f32[2048]{0:T(1024)}) all-reduce(f32[2048]{0:T(1024)S(1)} %get-tuple-element.53, f32[128]{0:T(128)S(1)} %reduce_sum.170, f32[128]{0:T(128)S(1)} %get-tuple-element.65, f32[2048]{0:T(1024)S(1)} %get-tuple-element.51), channel_id=1, replica_groups=mesh['dp'=8,'tensor'=4] {'dp','tensor'}, use_global_device_ids=true, to_apply=%region_19.20 | all-reduce | flops 4352 | bytes 34816 | tf_op jit(solution)/shard_map/psum | solution.py:379
  1148.8 13.7 %reduce-scatter.14.cloned.1.call-done = bf16[256,2048]{1,0:T(8,128)(2,1)} async-done(((bf16[1024,2048]{1,0:T(8,128)(2,1)}), bf16[256,2048]{1,0:T(8,128)(2,1)}) %reduce-scatter.14.cloned.1.call-update) | async-done | bytes 1048592 | tf_op jit(solution)/shard_map/reduce_scatter | solution.py:232
  1162.5 5.0 fusion.15
  (238 shorter events, 49.1 us)
Async XLA Ops:
  7.2 6.4 copy-start.5
  7.2 6.4 copy-start.53
  7.2 82.6 %all-gather.13.cloned.1.call-start = ((), (), s32[]{:S(2)}) async-start(), calls=%async_computation.12 | async-start | bytes 1179648 | tf_op jit(solution)/shard_map/all_gather | solution.py:138
  7.9 87.6 %all-gather.11.cloned.1.call-start = ((), (), s32[]{:S(2)}) async-start(), calls=%async_computation.11 | async-start | bytes 1179648 | tf_op jit(solution)/shard_map/all_gather | solution.py:139
  8.7 91.7 %all-gather.15.cloned.1.call-start = ((), (), s32[]{:S(2)}) async-start(), calls=%async_computation.13 | async-start | bytes 2359296 | tf_op jit(solution)/shard_map/all_gather | solution.py:137
  9.4 112.0 %all-gather.17.cloned.1.call-start = ((), (), s32[]{:S(2)}) async-start(), calls=%async_computation.14 | async-start | bytes 2359296 | tf_op jit(solution)/shard_map/all_gather | solution.py:140
  11.0 33.4 %copy-start.55 = (f32[256]{0:T(256)}, f32[256]{0:T(256)S(1)}, u32[]{:S(2)}) copy-start(f32[256]{0:T(256)S(1)} %add_rsqrt_fusion.3) | copy-start | bytes 3076
  15.2 28.1 %collective-permute-start = (bf16[256,2048]{1,0:T(8,128)(2,1)}, bf16[256,2048]{1,0:T(8,128)(2,1)S(1)}, u32[]{:S(2)}, u32[]{:S(2)}) collective-permute-start(bf16[256,2048]{1,0:T(8,128)(2,1)} %get-tuple-element.79), channel_id=1, source_target_pairs={{0,1},{1,2},{2,3},{3,0},{4,5},{5,6},{6,7},{7,4},{8,9},{9,10},{10,1... | collective-permute-start | bytes 3145736 | tf_op jit(solution)/shard_map/ppermute | solution.py:167
  18.2 48.2 %collective-permute-start.1 = (bf16[256,2048]{1,0:T(8,128)(2,1)}, bf16[256,2048]{1,0:T(8,128)(2,1)}, u32[]{:S(2)}, u32[]{:S(2)}) collective-permute-start(bf16[256,2048]{1,0:T(8,128)(2,1)} %get-tuple-element.79), channel_id=1, source_target_pairs={{0,3},{1,0},{2,1},{3,2},{4,7},{5,4},{6,5},{7,6},{8,11},{9,8},{10,9... | collective-permute-start | bytes 3145736 | tf_op jit(solution)/shard_map/ppermute | solution.py:172
  19.1 197.1 %reduce-scatter.12.cloned.1.call-start = ((), (), s32[]{:S(2)}) async-start(), calls=%async_computation.15 | async-start | bytes 10485760 | tf_op jit(solution)/shard_map/reduce_scatter | solution.py:214
  43.3 44.2 %collective-permute-start.2 = (bf16[256,2048]{1,0:T(8,128)(2,1)S(1)}, bf16[256,2048]{1,0:T(8,128)(2,1)}, u32[]{:S(2)}, u32[]{:S(2)}) collective-permute-start(bf16[256,2048]{1,0:T(8,128)(2,1)S(1)} %collective-permute-done), channel_id=1, source_target_pairs={{0,1},{1,2},{2,3},{3,0},{4,5},{5,6},{6,7},{7,4},{8,9},{9,10},{10,1... | collective-permute-start | bytes 3145736 | tf_op jit(solution)/shard_map/ppermute | solution.py:167
  47.3 46.7 %copy-start.9 = (f32[1024,128]{0,1:T(8,128)}, f32[1024,128]{0,1:T(8,128)S(1)}, u32[]{:S(2)}) copy-start(f32[1024,128]{0,1:T(8,128)S(1)} %get-tuple-element.99) | copy-start | bytes 1572868
  47.3 46.7 %copy-start.15 = (f32[1024,128]{0,1:T(8,128)}, f32[1024,128]{0,1:T(8,128)S(1)}, u32[]{:S(2)}) copy-start(f32[1024,128]{0,1:T(8,128)S(1)} %get-tuple-element.100) | copy-start | bytes 1572868
  89.8 3.9 copy-start.59
  93.6 6.8 copy-start.7
  100.4 5.3 copy-start.57
  108.6 4.1 copy-start.31
  110.6 5.7 copy-start.3
  114.5 4.3 copy-start.4
  121.3 7.9 copy-start.38
  121.4 7.7 copy-start.42
  129.2 89.0 %copy-start.52 = (f32[2048]{0:T(1024)S(1)}, f32[2048]{0:T(1024)}, u32[]{:S(2)}) copy-start(f32[2048]{0:T(1024)} %param.21) | copy-start | bytes 24580
  129.2 153.3 %all-gather.21.cloned.1.call-start = ((), (), s32[]{:S(2)}) async-start(), calls=%async_computation.17 | async-start | bytes 7077888 | tf_op jit(solution)/shard_map/all_gather | solution.py:141
  129.8 206.4 %all-gather.19.cloned.1.call-start = ((), (), s32[]{:S(2)}) async-start(), calls=%async_computation.16 | async-start | bytes 5242880 | tf_op jit(solution)/shard_map/all_gather | solution.py:227
  219.4 183.1 %all-gather.23.cloned.1.call-start = ((), (), s32[]{:S(2)}) async-start(), calls=%async_computation.18 | async-start | bytes 7077888 | tf_op jit(solution)/shard_map/all_gather | solution.py:142
  220.2 235.4 %all-gather.27.cloned.1.call-start = ((), (), s32[]{:S(2)}) async-start(), calls=%async_computation.21 | async-start | bytes 5242880 | tf_op jit(solution)/shard_map/all_gather | solution.py:252
  220.9 301.3 %all-gather.25.cloned.1.call-start = ((), (), s32[]{:S(2)}) async-start(), calls=%async_computation.19 | async-start | bytes 7077888 | tf_op jit(solution)/shard_map/all_gather | solution.py:143
  221.5 421.8 %reduce-scatter.16.cloned.1.call-start = ((), (), s32[]{:S(2)}) async-start(), calls=%async_computation.22 | async-start | bytes 10485760 | tf_op jit(solution)/shard_map/reduce_scatter | solution.py:263
  538.1 11.1 copy-start.65
  538.1 11.2 copy-start.66
  538.1 11.2 copy-start.61
  558.7 87.0 %copy-start.24 = (bf16[256,2048]{1,0:T(8,128)(2,1)S(1)}, bf16[256,2048]{1,0:T(8,128)(2,1)}, u32[]{:S(2)}) copy-start(bf16[256,2048]{1,0:T(8,128)(2,1)} %param.25) | copy-start | bytes 3145732
  558.7 141.4 %all-gather.29.cloned.1.call-start = ((), (), s32[]{:S(2)}) async-start(), calls=%async_computation.23 | async-start | bytes 5242880 | tf_op jit(solution)/shard_map/all_gather | solution.py:276
  647.3 153.1 %reduce-scatter.28.cloned.1.call-start = ((), (), s32[]{:S(2)}) async-start(), calls=%async_computation.29 | async-start | bytes 7077888 | tf_op jit(solution)/shard_map/reduce_scatter | solution.py:369
  659.0 183.6 %reduce-scatter.30.cloned.1.call-start = ((), (), s32[]{:S(2)}) async-start(), calls=%async_computation.30 | async-start | bytes 7077888 | tf_op jit(solution)/shard_map/reduce_scatter | solution.py:372
  670.5 242.4 %reduce-scatter.32.cloned.1.call-start = ((), (), s32[]{:S(2)}) async-start(), calls=%async_computation.31 | async-start | bytes 7077888 | tf_op jit(solution)/shard_map/reduce_scatter | solution.py:375
  681.8 23.6 %copy-start.37 = (bf16[512,2,2,128]{0,3,2,1:T(8,128)(2,1)S(1)}, bf16[512,2,2,128]{0,3,2,1:T(8,128)(2,1)}, u32[]{:S(2)}) copy-start(bf16[512,2,2,128]{0,3,2,1:T(8,128)(2,1)} %copy-done.36) | copy-start | bytes 1572868
  681.9 264.3 %reduce-scatter.24.cloned.1.call-start = ((), (), s32[]{:S(2)}) async-start(), calls=%async_computation.27 | async-start | bytes 1179648 | tf_op jit(solution)/shard_map/reduce_scatter | solution.py:363
  700.1 7.0 copy-start.30
  700.1 13.7 %slice-start = ((s8[8388608]{0:T(1024)(128)(4,1)}), s8[4194304]{0:T(1024)(128)(4,1)S(1)}, s32[]{:S(2)}) async-start(s8[8388608]{0:T(1024)(128)(4,1)} %bitcast.224), calls=%async_computation.32 | async-start | bytes 8388608
  705.5 8.3 slice-start.1
  707.1 6.7 copy-start.47
  707.1 6.7 copy-start.45
  707.1 6.7 copy-start.28
  721.8 8.6 copy-start.46
  721.8 8.7 copy-start.64
  730.4 6.9 copy-start.33
  737.3 241.8 %reduce-scatter.22.cloned.1.call-start = ((), (), s32[]{:S(2)}) async-start(), calls=%async_computation.26 | async-start | bytes 1179648 | tf_op jit(solution)/shard_map/reduce_scatter | solution.py:360
  737.3 3.9 copy-start.21
  750.5 6.7 copy-start.58
  750.5 6.7 copy-start.49
  750.6 265.0 %reduce-scatter.26.cloned.1.call-start = ((), (), s32[]{:S(2)}) async-start(), calls=%async_computation.28 | async-start | bytes 2359296 | tf_op jit(solution)/shard_map/reduce_scatter | solution.py:366
  756.9 295.6 %reduce-scatter.20.cloned.1.call-start = ((), (), s32[]{:S(2)}) async-start(), calls=%async_computation.25 | async-start | bytes 2359296 | tf_op jit(solution)/shard_map/reduce_scatter | solution.py:357
  757.3 3.7 copy-start.18
  757.3 3.8 copy-start.23
  763.6 3.3 copy-start.25
  763.7 3.2 copy-start.26
  767.0 2.9 copy-start.14
  774.2 6.0 copy-start.35
  780.2 326.4 %reduce-scatter.18.cloned.1.call-start = ((), (), s32[]{:S(2)}) async-start(), calls=%async_computation.24 | async-start | bytes 5242880 | tf_op jit(solution)/shard_map/reduce_scatter | solution.py:336
  788.8 373.6 %reduce-scatter.14.cloned.1.call-start = ((), (), s32[]{:S(2)}) async-start(), calls=%async_computation.20 | async-start | bytes 5242880 | tf_op jit(solution)/shard_map/reduce_scatter | solution.py:232
  800.4 306.2 %copy-start.6 = (bf16[256,2048]{1,0:T(8,128)(2,1)S(1)}, bf16[256,2048]{1,0:T(8,128)(2,1)}, u32[]{:S(2)}) copy-start(bf16[256,2048]{1,0:T(8,128)(2,1)} %param.13) | copy-start | bytes 3145732
  800.4 306.2 %copy-start.54 = (f32[2048]{0:T(1024)S(1)}, f32[2048]{0:T(1024)}, u32[]{:S(2)}) copy-start(f32[2048]{0:T(1024)} %param.14) | copy-start | bytes 24580
  800.4 306.2 %copy-start.56 = (f32[256]{0:T(256)S(1)}, f32[256]{0:T(256)}, u32[]{:S(2)}) copy-start(f32[256]{0:T(256)} %copy-done.55) | copy-start | bytes 3076
  (29 other events, 57.8 us)
Sparse Core Ops, SparseCore 0:
  9.6 24.9 all-gather.12
  36.2 21.8 all-gather.10
  59.7 28.7 all-gather.14
  89.9 30.0 all-gather.16
  129.3 86.8 reduce-scatter.11
  217.7 64.6 all-gather.20
  284.9 51.2 all-gather.18
  337.8 64.6 all-gather.22
  404.3 51.2 all-gather.26
  457.0 65.1 all-gather.24
  558.8 84.4 reduce-scatter.15
  647.5 52.5 all-gather.28
  702.4 69.7 reduce-scatter.27
  774.3 68.1 reduce-scatter.29
  844.7 68.1 reduce-scatter.31
  915.0 31.0 reduce-scatter.23
  948.2 30.7 reduce-scatter.21
  981.2 34.2 reduce-scatter.25
  1017.8 34.6 reduce-scatter.19
  1055.4 51.2 reduce-scatter.17
  1109.6 52.8 reduce-scatter.13
